TPU v7x, 32 devices: a whole 2x2x4 slice. The times are simulated.
32 devices in a mesh: rows: 4 (over z), cols: 2 (over x), slabs: 4 (over y, core).
Axes of the slice: x: 2, y: 2, z: 4, core: 2. Of those that a mesh axis runs over, the one named last changes fastest.
Arguments:
- pressure: float32 [512, 8, 128, 128], P('rows', 'cols', 'slabs'), may hold values from 0.5 to 2
- earlier: float32 [512, 8, 128, 128], P('rows', 'cols', 'slabs'), may hold values from 0.2 to 1.8
- speed_square: float32 [512, 8, 128, 128], P('rows', 'cols', 'slabs'), may hold values from 0.05 to 0.3
Outputs:
- scaled_field: float32 [512, 8, 128, 128], P('rows', 'cols', 'slabs')
- pressure_end: float32 [512, 8, 128, 128], P('rows', 'cols', 'slabs')
All inputs are finite; a program needn't handle non-finite values.
Results may differ from a plain program's by a relative error of at most 0.00002.
Values sent between devices are 32-bit elements; how exact they have to be, the bound alone decides.
A program may use at most 128 MiB of HBM per device.

v0:
```python
import jax
import jax.numpy as jnp
from jax import lax
from jax.sharding import PartitionSpec as P

STEPS = 3


def padded_2(shard, sides, width):
    for axis, dim in sides:
        count, length = (lax.axis_size(axis), shard.shape[dim])
        up = [(i, (i + 1) % count) for i in range(count)]
        down = [(j, i) for i, j in up]
        last = lax.slice_in_dim(shard, length - width, length, axis=dim)
        initial = lax.slice_in_dim(shard, 0, width, axis=dim)
        before = lax.ppermute(last, axis, up)
        after = lax.ppermute(initial, axis, down)
        shard = jnp.concatenate([before, shard, after], axis=dim)
    return shard


def strip_edges(values, dims):
    for dim in dims:
        values = lax.slice_in_dim(values, 1, values.shape[dim] - 1, axis=dim)
    return values


def neighbour(values, dim, start, dims):
    others = [other for other in dims if other != dim]
    values = strip_edges(values, others)
    return lax.slice_in_dim(values, start, start + values.shape[dim] - 2, axis=dim)


def one_step(padded, before, speed_square):
    middle = strip_edges(padded, (0, 1, 2))
    lower = [neighbour(padded, dim, 0, (0, 1, 2)) for dim in (0, 1, 2)]
    upper = [neighbour(padded, dim, 2, (0, 1, 2)) for dim in (0, 1, 2)]
    spread = lower[0] + upper[0] + lower[1] + upper[1] + lower[2] + upper[2] - 6.0 * middle
    return 2.0 * middle - before + speed_square * spread


def shards(pressure, earlier, speed_square):
    for step in range(STEPS):
        padded = padded_2(pressure, (("rows", 0), ("cols", 1), ("slabs", 2)), 1)
        later = one_step(padded, earlier, speed_square)
        earlier, pressure = (pressure, later)
    count = pressure.shape[0] * lax.axis_size("rows")
    guess = 1.0
    moved = pressure - guess
    totals, squares = lax.psum(
        (jnp.sum(moved, axis=0, keepdims=True), jnp.sum(moved * moved, axis=0, keepdims=True)),
        "rows",
    )
    line_mean = guess + totals / count
    centred = pressure - line_mean
    line_variance = squares / count - totals / count * (totals / count)
    scaled_field = centred * lax.rsqrt(line_variance + 0.0001)
    return (scaled_field, pressure)


def solution(mesh):
    in_specs = (
        P("rows", "cols", "slabs", None),
        P("rows", "cols", "slabs", None),
        P("rows", "cols", "slabs", None),
    )
    out_specs = (P("rows", "cols", "slabs", None), P("rows", "cols", "slabs", None))
    return jax.shard_map(shards, mesh=mesh, in_specs=in_specs, out_specs=out_specs, check_vma=False)
```

profile of v0, /device:TPU:0, one launch (start us, length us, event | category | flops | bytes accessed | tf_op | source)
XLA Modules:
  0.0 517.5 jit_solution(14439541878618777186)
XLA Ops:
  8.1 3.1 collective-permute-start
  11.2 2.1 collective-permute-start.1
  13.3 2.3 collective-permute-done
  15.6 4.4 constant_dynamic-update-slice_fusion.1
  20.6 2.0 collective-permute-start.2
  22.7 47.2 %collective-permute-done.2 = f32[130,1,32,128]{3,2,1,0:T(8,128)S(1)} collective-permute-done((f32[130,1,32,128]{3,2,1,0:T(8,128)S(1)}, f32[130,1,32,128]{3,2,1,0:T(8,128)S(1)}, u32[]{:S(2)}, u32[]{:S(2)}) %collective-permute-start.2) | collective-permute-done | bytes 2129952 | tf_op jit(solution)/shard_map/ppermute | solution.py:16
  69.9 43.6 %collective-permute-done.3 = f32[130,1,32,128]{3,2,1,0:T(8,128)S(1)} collective-permute-done((f32[130,1,32,128]{3,2,1,0:T(8,128)S(1)}, f32[130,1,32,128]{3,2,1,0:T(8,128)S(1)}, u32[]{:S(2)}, u32[]{:S(2)}) %collective-permute-start.3) | collective-permute-done | bytes 2129952 | tf_op jit(solution)/shard_map/ppermute | solution.py:17
  114.8 8.4 %collective-permute-done.5 = f32[130,6,1,128]{3,0,2,1:T(8,128)S(1)} collective-permute-done((f32[130,6,1,128]{3,0,2,1:T(8,128)S(1)}, f32[130,6,1,128]{3,0,2,1:T(8,128)S(1)}, u32[]{:S(2)}, u32[]{:S(2)}) %collective-permute-start.5) | collective-permute-done | bytes 399392 | tf_op jit(solution)/shard_map/ppermute | solution.py:17
  123.6 2.6 collective-permute-done.4
  126.6 31.5 %fusion.19 = f32[128,4,32,128]{3,2,1,0:T(8,128)} fusion(f32[128,4,32,128]{3,2,1,0:T(8,128)} %param.5, f32[130,6,1,128]{3,2,1,0:T(1,128)S(1)} %copy.22, f32[130,1,32,128]{3,2,1,0:T(8,128)S(1)} %collective-permute-done.3, f32[130,4,32,128]{3,2,1,0:T(8,128)} %copy-done.2, f32[130,1,32,128]{3,2,1,0:T(8,128)S(1)} %collective-permute-done.2, ...), kind=kLoop, calls=%fused_computation.56 | loop fusion | flops 44040192 | bytes 47263744 | tf_op jit(solution)/shard_map/add | solution.py:39
  158.1 1.0 fusion.27
  159.2 3.8 collective-permute-start.7
  163.1 2.9 collective-permute-done.6
  166.0 2.7 pad_maximum_fusion.51
  168.7 1.6 collective-permute-start.8
  170.8 47.2 %collective-permute-done.8 = f32[130,1,32,128]{3,2,1,0:T(8,128)S(1)} collective-permute-done((f32[130,1,32,128]{3,2,1,0:T(8,128)S(1)}, f32[130,1,32,128]{3,2,1,0:T(8,128)S(1)}, u32[]{:S(2)}, u32[]{:S(2)}) %collective-permute-start.8) | collective-permute-done | bytes 2129952 | tf_op jit(solution)/shard_map/ppermute | solution.py:16
  218.0 43.9 %collective-permute-done.9 = f32[130,1,32,128]{3,2,1,0:T(8,128)S(1)} collective-permute-done((f32[130,1,32,128]{3,2,1,0:T(8,128)S(1)}, f32[130,1,32,128]{3,2,1,0:T(8,128)S(1)}, u32[]{:S(2)}, u32[]{:S(2)}) %collective-permute-start.9) | collective-permute-done | bytes 2129952 | tf_op jit(solution)/shard_map/ppermute | solution.py:17
  261.9 1.1 pad_maximum_fusion.61
  263.8 9.2 %collective-permute-done.11 = f32[130,6,1,128]{3,0,2,1:T(8,128)S(1)} collective-permute-done((f32[130,6,1,128]{3,0,2,1:T(8,128)S(1)}, f32[130,6,1,128]{3,0,2,1:T(8,128)S(1)}, u32[]{:S(2)}, u32[]{:S(2)}) %collective-permute-start.11) | collective-permute-done | bytes 399392 | tf_op jit(solution)/shard_map/ppermute | solution.py:17
  273.9 36.6 %fusion.11 = f32[128,4,32,128]{3,2,1,0:T(8,128)} fusion(f32[128,4,32,128]{3,2,1,0:T(8,128)} %param.5, f32[130,6,1,128]{3,2,1,0:T(1,128)S(1)} %copy.26, f32[130,1,32,128]{3,2,1,0:T(8,128)S(1)} %collective-permute-done.9, f32[130,1,32,128]{3,2,1,0:T(8,128)S(1)} %collective-permute-done.8, f32[1,4,32,128]{3,2,1,0:T(8,128)S(1)} %collective-permute-done.7, ...), kind=kLoop, calls=%fused_computation.30 | loop fusion | flops 60817408 | bytes 38744064 | tf_op jit(solution)/shard_map/add | solution.py:39
  311.6 3.8 collective-permute-start.13
  315.4 2.7 collective-permute-done.12
  318.1 2.7 pad_maximum_fusion.48
  320.8 1.6 collective-permute-start.14
  322.9 47.2 %collective-permute-done.14 = f32[130,1,32,128]{3,2,1,0:T(8,128)S(1)} collective-permute-done((f32[130,1,32,128]{3,2,1,0:T(8,128)S(1)}, f32[130,1,32,128]{3,2,1,0:T(8,128)S(1)}, u32[]{:S(2)}, u32[]{:S(2)}) %collective-permute-start.14) | collective-permute-done | bytes 2129952 | tf_op jit(solution)/shard_map/ppermute | solution.py:16
  370.1 43.0 %collective-permute-done.15 = f32[130,1,32,128]{3,2,1,0:T(8,128)S(1)} collective-permute-done((f32[130,1,32,128]{3,2,1,0:T(8,128)S(1)}, f32[130,1,32,128]{3,2,1,0:T(8,128)S(1)}, u32[]{:S(2)}, u32[]{:S(2)}) %collective-permute-start.15) | collective-permute-done | bytes 2129952 | tf_op jit(solution)/shard_map/ppermute | solution.py:17
  413.1 1.1 pad_maximum_fusion.56
  415.5 7.8 %collective-permute-done.17 = f32[130,6,1,128]{3,0,2,1:T(8,128)S(1)} collective-permute-done((f32[130,6,1,128]{3,0,2,1:T(8,128)S(1)}, f32[130,6,1,128]{3,0,2,1:T(8,128)S(1)}, u32[]{:S(2)}, u32[]{:S(2)}) %collective-permute-start.17) | collective-permute-done | bytes 399392 | tf_op jit(solution)/shard_map/ppermute | solution.py:17
  423.8 4.1 collective-permute-done.16
  428.3 38.0 %add_reduce_fusion = (f32[4,32,128]{2,1,0:T(8,128)}, f32[4,32,128]{2,1,0:T(8,128)}, f32[128,4,32,128]{3,2,1,0:T(8,128)}) fusion(f32[128,4,32,128]{3,2,1,0:T(8,128)} %param.5, f32[128,4,32,128]{3,2,1,0:T(8,128)} %fusion.11, f32[130,6,1,128]{3,2,1,0:T(1,128)S(1)} %copy.30, f32[130,1,32,128]{3,2,1,0:T(8,128)S(1)} %collective-permute-done.15, ...), kind=kLoop, calls=%fused_computation.72 | loop fusion | flops 69173248 | bytes 38875136 | tf_op jit(solution)/shard_map/reduce_sum | solution.py:51
  466.3 34.7 %all-reduce.3.cloned.1.call-done = (f32[1,4,32,128]{3,2,1,0:T(8,128)}, f32[1,4,32,128]{3,2,1,0:T(8,128)}) async-done(((f32[1,4,32,128]{3,2,1,0:T(8,128)}, f32[1,4,32,128]{3,2,1,0:T(8,128)}), (f32[1,4,32,128]{3,2,1,0:T(8,128)}, f32[1,4,32,128]{3,2,1,0:T(8,128)})) %all-reduce.3.cloned.1.call-update) | async-done | bytes 131088 | tf_op jit(solution)/shard_map/psum | solution.py:50
  501.8 8.8 %subtract_multiply_fusion = f32[128,4,32,128]{3,2,1,0:T(8,128)} fusion(f32[128,4,32,128]{3,2,1,0:T(8,128)} %get-tuple-element.8, f32[4,32,128]{2,1,0:T(8,128)S(1)} %get-tuple-element.28, f32[4,32,128]{2,1,0:T(8,128)S(1)} %get-tuple-element.27), kind=kLoop, calls=%fused_computation.71 | loop fusion | flops 4194304 | bytes 16908288 | tf_op jit(solution)/shard_map/mul | solution.py:57
  (42 shorter events, 10.7 us)
Async XLA Ops:
  7.2 493.8 %all-reduce.3.cloned.1.call-start = ((), (), s32[]{:S(2)}) async-start(), calls=%async_computation | async-start | bytes 262144 | tf_op jit(solution)/shard_map/psum | solution.py:50
  8.1 7.5 %collective-permute-start = (f32[1,4,32,128]{3,2,1,0:T(8,128)S(1)}, f32[1,4,32,128]{3,2,1,0:T(8,128)S(1)}, u32[]{:S(2)}, u32[]{:S(2)}) collective-permute-start(f32[1,4,32,128]{3,2,1,0:T(8,128)S(1)} %get-tuple-element.26), channel_id=1, source_target_pairs={{0,8},{8,16},{16,24},{24,0},{1,9},{9,17},{17,25},{25,1},{2,10},{10... | collective-permute-start | bytes 196616 | tf_op jit(solution)/shard_map/ppermute | solution.py:16
  11.2 8.8 %collective-permute-start.1 = (f32[1,4,32,128]{3,2,1,0:T(8,128)S(1)}, f32[1,4,32,128]{3,2,1,0:T(8,128)S(1)}, u32[]{:S(2)}, u32[]{:S(2)}) collective-permute-start(f32[1,4,32,128]{3,2,1,0:T(8,128)S(1)} %get-tuple-element.25), channel_id=1, source_target_pairs={{8,0},{16,8},{24,16},{0,24},{9,1},{17,9},{25,17},{1,25},{10,2},{18... | collective-permute-start | bytes 196616 | tf_op jit(solution)/shard_map/ppermute | solution.py:17
  20.0 94.1 %copy-start.2 = (f32[130,4,32,128]{3,2,1,0:T(8,128)}, f32[130,4,32,128]{3,2,1,0:T(8,128)S(1)}, u32[]{:S(2)}) copy-start(f32[130,4,32,128]{3,2,1,0:T(8,128)S(1)} %constant_dynamic-update-slice_fusion) | copy-start | bytes 25559044
  20.6 49.3 %collective-permute-start.2 = (f32[130,1,32,128]{3,2,1,0:T(8,128)S(1)}, f32[130,1,32,128]{3,2,1,0:T(8,128)S(1)}, u32[]{:S(2)}, u32[]{:S(2)}) collective-permute-start(f32[130,1,32,128]{3,2,1,0:T(8,128)S(1)} %get-tuple-element.19), channel_id=1, source_target_pairs={{0,4},{4,0},{1,5},{5,1},{2,6},{6,2},{3,7},{7,3},{8,12},{12,8},{9,1... | collective-permute-start | bytes 6389768 | tf_op jit(solution)/shard_map/ppermute | solution.py:16
  22.6 90.9 %collective-permute-start.3 = (f32[130,1,32,128]{3,2,1,0:T(8,128)S(1)}, f32[130,1,32,128]{3,2,1,0:T(8,128)S(1)}, u32[]{:S(2)}, u32[]{:S(2)}) collective-permute-start(f32[130,1,32,128]{3,2,1,0:T(8,128)S(1)} %get-tuple-element.20), channel_id=1, source_target_pairs={{4,0},{0,4},{5,1},{1,5},{6,2},{2,6},{7,3},{3,7},{12,8},{8,12},{13,... | collective-permute-start | bytes 6389768 | tf_op jit(solution)/shard_map/ppermute | solution.py:17
  114.2 9.0 %collective-permute-start.5 = (f32[130,6,1,128]{3,0,2,1:T(8,128)S(1)}, f32[130,6,1,128]{3,0,2,1:T(8,128)S(1)}, u32[]{:S(2)}, u32[]{:S(2)}) collective-permute-start(f32[130,6,1,128]{3,0,2,1:T(8,128)S(1)} %copy.21), channel_id=1, source_target_pairs={{1,0},{2,1},{3,2},{0,3},{5,4},{6,5},{7,6},{4,7},{9,8},{10,9},{11,1... | collective-permute-start | bytes 1198088 | tf_op jit(solution)/shard_map/ppermute | solution.py:17
  114.3 12.0 %collective-permute-start.4 = (f32[130,6,1,128]{3,0,2,1:T(8,128)S(1)}, f32[130,6,1,128]{3,0,2,1:T(8,128)S(1)}, u32[]{:S(2)}, u32[]{:S(2)}) collective-permute-start(f32[130,6,1,128]{3,0,2,1:T(8,128)S(1)} %copy.19), channel_id=1, source_target_pairs={{0,1},{1,2},{2,3},{3,0},{4,5},{5,6},{6,7},{7,4},{8,9},{9,10},{10,1... | collective-permute-start | bytes 1198088 | tf_op jit(solution)/shard_map/ppermute | solution.py:16
  158.1 103.7 %copy-start = (f32[128,4,32,128]{3,2,1,0:T(8,128)S(1)}, f32[128,4,32,128]{3,2,1,0:T(8,128)}, u32[]{:S(2)}) copy-start(f32[128,4,32,128]{3,2,1,0:T(8,128)} %fusion.19) | copy-start | bytes 25165828
  159.2 6.8 %collective-permute-start.6 = (f32[1,4,32,128]{3,2,1,0:T(8,128)S(1)}, f32[1,4,32,128]{3,2,1,0:T(8,128)S(1)}, u32[]{:S(2)}, u32[]{:S(2)}) collective-permute-start(f32[1,4,32,128]{3,2,1,0:T(8,128)S(1)} %get-tuple-element.23), channel_id=1, source_target_pairs={{0,8},{8,16},{16,24},{24,0},{1,9},{9,17},{17,25},{25,1},{2,10},{10... | collective-permute-start | bytes 196616 | tf_op jit(solution)/shard_map/ppermute | solution.py:16
  159.2 6.8 %collective-permute-start.7 = (f32[1,4,32,128]{3,2,1,0:T(8,128)S(1)}, f32[1,4,32,128]{3,2,1,0:T(8,128)S(1)}, u32[]{:S(2)}, u32[]{:S(2)}) collective-permute-start(f32[1,4,32,128]{3,2,1,0:T(8,128)S(1)} %get-tuple-element.24), channel_id=1, source_target_pairs={{8,0},{16,8},{24,16},{0,24},{9,1},{17,9},{25,17},{1,25},{10,2},{18... | collective-permute-start | bytes 196616 | tf_op jit(solution)/shard_map/ppermute | solution.py:17
  168.7 49.3 %collective-permute-start.8 = (f32[130,1,32,128]{3,2,1,0:T(8,128)S(1)}, f32[130,1,32,128]{3,2,1,0:T(8,128)S(1)}, u32[]{:S(2)}, u32[]{:S(2)}) collective-permute-start(f32[130,1,32,128]{3,2,1,0:T(8,128)S(1)} %get-tuple-element.17), channel_id=1, source_target_pairs={{0,4},{4,0},{1,5},{5,1},{2,6},{6,2},{3,7},{7,3},{8,12},{12,8},{9,1... | collective-permute-start | bytes 6389768 | tf_op jit(solution)/shard_map/ppermute | solution.py:16
  170.3 91.6 %collective-permute-start.9 = (f32[130,1,32,128]{3,2,1,0:T(8,128)S(1)}, f32[130,1,32,128]{3,2,1,0:T(8,128)S(1)}, u32[]{:S(2)}, u32[]{:S(2)}) collective-permute-start(f32[130,1,32,128]{3,2,1,0:T(8,128)S(1)} %get-tuple-element.18), channel_id=1, source_target_pairs={{4,0},{0,4},{5,1},{1,5},{6,2},{2,6},{7,3},{3,7},{12,8},{8,12},{13,... | collective-permute-start | bytes 6389768 | tf_op jit(solution)/shard_map/ppermute | solution.py:17
  263.0 10.0 %collective-permute-start.11 = (f32[130,6,1,128]{3,0,2,1:T(8,128)S(1)}, f32[130,6,1,128]{3,0,2,1:T(8,128)S(1)}, u32[]{:S(2)}, u32[]{:S(2)}) collective-permute-start(f32[130,6,1,128]{3,0,2,1:T(8,128)S(1)} %copy.25), channel_id=1, source_target_pairs={{1,0},{2,1},{3,2},{0,3},{5,4},{6,5},{7,6},{4,7},{9,8},{10,9},{11,1... | collective-permute-start | bytes 1198088 | tf_op jit(solution)/shard_map/ppermute | solution.py:17
  263.1 10.4 %collective-permute-start.10 = (f32[130,6,1,128]{3,0,2,1:T(8,128)S(1)}, f32[130,6,1,128]{3,0,2,1:T(8,128)S(1)}, u32[]{:S(2)}, u32[]{:S(2)}) collective-permute-start(f32[130,6,1,128]{3,0,2,1:T(8,128)S(1)} %copy.23), channel_id=1, source_target_pairs={{0,1},{1,2},{2,3},{3,0},{4,5},{5,6},{6,7},{7,4},{8,9},{9,10},{10,1... | collective-permute-start | bytes 1198088 | tf_op jit(solution)/shard_map/ppermute | solution.py:16
  310.5 102.6 %copy-start.1 = (f32[128,4,32,128]{3,2,1,0:T(8,128)S(1)}, f32[128,4,32,128]{3,2,1,0:T(8,128)}, u32[]{:S(2)}) copy-start(f32[128,4,32,128]{3,2,1,0:T(8,128)} %fusion.11) | copy-start | bytes 25165828
  311.5 6.6 %collective-permute-start.12 = (f32[1,4,32,128]{3,2,1,0:T(8,128)S(1)}, f32[1,4,32,128]{3,2,1,0:T(8,128)S(1)}, u32[]{:S(2)}, u32[]{:S(2)}) collective-permute-start(f32[1,4,32,128]{3,2,1,0:T(8,128)S(1)} %get-tuple-element.21), channel_id=1, source_target_pairs={{0,8},{8,16},{16,24},{24,0},{1,9},{9,17},{17,25},{25,1},{2,10},{10... | collective-permute-start | bytes 196616 | tf_op jit(solution)/shard_map/ppermute | solution.py:16
  311.6 6.5 %collective-permute-start.13 = (f32[1,4,32,128]{3,2,1,0:T(8,128)S(1)}, f32[1,4,32,128]{3,2,1,0:T(8,128)S(1)}, u32[]{:S(2)}, u32[]{:S(2)}) collective-permute-start(f32[1,4,32,128]{3,2,1,0:T(8,128)S(1)} %get-tuple-element.22), channel_id=1, source_target_pairs={{8,0},{16,8},{24,16},{0,24},{9,1},{17,9},{25,17},{1,25},{10,2},{18... | collective-permute-start | bytes 196616 | tf_op jit(solution)/shard_map/ppermute | solution.py:17
  320.8 49.3 %collective-permute-start.14 = (f32[130,1,32,128]{3,2,1,0:T(8,128)S(1)}, f32[130,1,32,128]{3,2,1,0:T(8,128)S(1)}, u32[]{:S(2)}, u32[]{:S(2)}) collective-permute-start(f32[130,1,32,128]{3,2,1,0:T(8,128)S(1)} %get-tuple-element.15), channel_id=1, source_target_pairs={{0,4},{4,0},{1,5},{5,1},{2,6},{6,2},{3,7},{7,3},{8,12},{12,8},{9,1... | collective-permute-start | bytes 6389768 | tf_op jit(solution)/shard_map/ppermute | solution.py:16
  322.4 90.7 %collective-permute-start.15 = (f32[130,1,32,128]{3,2,1,0:T(8,128)S(1)}, f32[130,1,32,128]{3,2,1,0:T(8,128)S(1)}, u32[]{:S(2)}, u32[]{:S(2)}) collective-permute-start(f32[130,1,32,128]{3,2,1,0:T(8,128)S(1)} %get-tuple-element.16), channel_id=1, source_target_pairs={{4,0},{0,4},{5,1},{1,5},{6,2},{2,6},{7,3},{3,7},{12,8},{8,12},{13,... | collective-permute-start | bytes 6389768 | tf_op jit(solution)/shard_map/ppermute | solution.py:17
  414.2 9.1 %collective-permute-start.17 = (f32[130,6,1,128]{3,0,2,1:T(8,128)S(1)}, f32[130,6,1,128]{3,0,2,1:T(8,128)S(1)}, u32[]{:S(2)}, u32[]{:S(2)}) collective-permute-start(f32[130,6,1,128]{3,0,2,1:T(8,128)S(1)} %copy.29), channel_id=1, source_target_pairs={{1,0},{2,1},{3,2},{0,3},{5,4},{6,5},{7,6},{4,7},{9,8},{10,9},{11,1... | collective-permute-start | bytes 1198088 | tf_op jit(solution)/shard_map/ppermute | solution.py:17
  415.3 12.6 %collective-permute-start.16 = (f32[130,6,1,128]{3,0,2,1:T(8,128)S(1)}, f32[130,6,1,128]{3,0,2,1:T(8,128)S(1)}, u32[]{:S(2)}, u32[]{:S(2)}) collective-permute-start(f32[130,6,1,128]{3,0,2,1:T(8,128)S(1)} %copy.27), channel_id=1, source_target_pairs={{0,1},{1,2},{2,3},{3,0},{4,5},{5,6},{6,7},{7,4},{8,9},{9,10},{10,1... | collective-permute-start | bytes 1198088 | tf_op jit(solution)/shard_map/ppermute | solution.py:16
Sparse Core Ops, SparseCore 0:
  466.4 34.4 all-reduce.2
where the time goes:
time: 518 us
  waiting for transfers between devices  347 us (67%)
  other arithmetic  124 us (24%)
  starting transfers between devices  21.9 us (4%)
  between operations  14.2 us (3%)
  local copies, waits for them, and re-layouts  10.6 us (2%)
    ppermute x9, waiting for transfers between devices, padded_2(): before = lax.ppermute(last, axis, up)  156 us
    ppermute x9, waiting for transfers between devices, padded_2(): after = lax.ppermute(initial, axis, down)  156 us
    add x2, other arithmetic, one_step(): return 2.0 * middle - before + speed_square * spread  68.1 us
    reduce_sum x1, other arithmetic, shards(): jnp.sum(moved, axis=0, keepdims=True)  38 us
    psum x1, waiting for transfers between devices, shards(): lax.psum((jnp.sum(moved, axis=0, keepdims=True), jnp.sum(moved * moved, a...  34.7 us
    ppermute x9, starting transfers between devices, padded_2(): after = lax.ppermute(initial, axis, down)  12 us
  transfers between devices with their start and end apart: 19, of which 16 were waited for; matrix products, arithmetic and copies ran while one was open for 1% of the time, Pallas kernels for 0%

commit v1 on v0

v1 whole, which is shorter than its diff:
```python
import functools

import jax
import jax.numpy as jnp
from jax import lax
from jax.experimental import pallas as pl
from jax.experimental.pallas import tpu as pltpu
from jax.sharding import PartitionSpec as P

STEPS = 3
GUESS = 1.0
EPS = 0.0001
MESH = pl.DeviceIdType.MESH
TILE = 8
LO, HI = 0, 1


def leapfrog(sizes, p_hbm, e_hbm, s_hbm, out_hbm, stat_hbm,
             even, odd, speed, xh, yh, line, stat,
             xs, xr, ys, yr, zs, zr, ls, lr, own, out_sem):
    rows, cols, slabs = sizes
    planes, cells, depth = p_hbm.shape[0], p_hbm.shape[1], p_hbm.shape[2]
    tiles = depth // TILE
    body_planes = pl.ds(1, planes)
    row, col, slab = (lax.axis_index(name) for name in ("rows", "cols", "slabs"))

    def shifted(name, index, count, by):
        return {name: lax.rem(index + by + count, count)}

    x_to = (shifted("cols", col, cols, -1), shifted("cols", col, cols, 1))
    y_to = (shifted("slabs", slab, slabs, -1), shifted("slabs", slab, slabs, 1))
    z_to = (shifted("rows", row, rows, -1), shifted("rows", row, rows, 1))
    peers = [shifted("rows", row, rows, d) for d in range(1, rows)]

    loads = [
        pltpu.make_async_copy(p_hbm, even.at[body_planes], own.at[0]),
        pltpu.make_async_copy(e_hbm, odd.at[body_planes], own.at[1]),
        pltpu.make_async_copy(s_hbm, speed, own.at[2]),
    ]
    for load in loads:
        load.start()

    barrier = pltpu.get_barrier_semaphore()
    greeted = list(x_to) + list(y_to) + peers
    for device in greeted:
        pl.semaphore_signal(barrier, inc=1, device_id=device, device_id_type=MESH)
    pl.semaphore_wait(barrier, len(greeted))

    fields = (even, odd)

    def remote(src, dst, send, recv, device):
        return pltpu.make_async_remote_copy(
            src_ref=src, dst_ref=dst, send_sem=send, recv_sem=recv,
            device_id=device, device_id_type=MESH,
        )

    def source(step):
        return p_hbm if step == 0 else fields[step % 2].at[body_planes]

    def x_copy(step, side, q):
        cell = 0 if side == LO else cells - 1
        part = pl.ds(q * TILE, TILE)
        return remote(source(step).at[:, cell, part, :], xh.at[step, 1 - side, :, part, :],
                      xs.at[step, side, q], xr.at[step, side, q], x_to[side])

    def y_copy(step, side):
        part = pl.ds(0 if side == LO else depth - TILE, TILE)
        return remote(source(step).at[:, :, part, :], yh.at[step, 1 - side],
                      ys.at[step, side], yr.at[step, side], y_to[side])

    def z_copy(step, side):
        src = p_hbm.at[0 if side == LO else planes - 1] if step == 0 else (
            fields[step % 2].at[1 if side == LO else planes])
        dst = fields[step % 2].at[planes + 1 if side == LO else 0]
        return remote(src, dst, zs.at[step, side], zr.at[step, side], z_to[side])

    def order(step):
        return (LO, HI) if step % 2 == 0 else (HI, LO)

    def update(step, cell, q, low, high):
        now, then = fields[step % 2], fields[(step + 1) % 2]
        part = pl.ds(q * TILE, TILE)
        index = lax.broadcasted_iota(jnp.int32, (TILE, TILE, 128), 1)
        last = step == STEPS - 1

        def block(b, sums):
            j = b * TILE
            here, padded = pl.ds(j, TILE), pl.ds(j + 1, TILE)
            mid = now[padded, cell, part, :]
            if q == 0:
                below = yh[step, LO, here, cell, TILE - 1:TILE, :]
            else:
                below = now[padded, cell, q * TILE - 1:q * TILE, :]
            if q == tiles - 1:
                above = yh[step, HI, here, cell, 0:1, :]
            else:
                above = now[padded, cell, (q + 1) * TILE:(q + 1) * TILE + 1, :]
            k_low = jnp.where(index == 0, below, pltpu.roll(mid, 1, 1))
            k_high = jnp.where(index == TILE - 1, above, pltpu.roll(mid, TILE - 1, 1))
            spread = (now[here, cell, part, :] + now[pl.ds(j + 2, TILE), cell, part, :]
                      + low(here, padded, part) + high(here, padded, part)
                      + k_low + k_high - 6.0 * mid)
            new = 2.0 * mid - then[padded, cell, part, :] + speed[here, cell, part, :] * spread
            then[padded, cell, part, :] = new
            if last:
                moved = new - GUESS
                return sums[0] + jnp.sum(moved, axis=0), sums[1] + jnp.sum(moved * moved, axis=0)
            return sums

        zero = jnp.zeros((TILE, 128), jnp.float32)
        sums = lax.fori_loop(0, planes // TILE, block, (zero, zero) if last else 0)
        if last:
            line[row, cell, 0, part, :] = sums[0]
            line[row, cell, 1, part, :] = sums[1]

    def edge(step, side, q):
        now = fields[step % 2]
        halo = lambda here, padded, part: xh[step, side, here, part, :]
        if side == LO:
            update(step, 0, q, halo, lambda here, padded, part: now[padded, 1, part, :])
        else:
            update(step, cells - 1, q, lambda here, padded, part: now[padded, cells - 2, part, :], halo)

    def interior(step):
        now = fields[step % 2]

        def at(cell, carry):
            for q in range(tiles):
                update(step, cell, q,
                       lambda here, padded, part: now[padded, cell - 1, part, :],
                       lambda here, padded, part: now[padded, cell + 1, part, :])
            return carry

        lax.fori_loop(1, cells - 1, at, 0)

    def line_copies(cell):
        return [remote(line.at[row, cell], line.at[row, cell], ls.at[cell, d], lr.at[cell, d], device)
                for d, device in enumerate(peers)]

    def out_copy(cell):
        return pltpu.make_async_copy(odd.at[body_planes, cell], out_hbm.at[:, cell], out_sem.at[cell])

    def finished(cell):
        out_copy(cell).start()
        for copy in line_copies(cell):
            copy.start()

    for side in order(0):
        for q in range(tiles):
            x_copy(0, side, q).start()
    for side in (LO, HI):
        z_copy(0, side).start()
        y_copy(0, side).start()
    for load in loads:
        load.wait()

    for step in range(STEPS):
        if step >= 1:
            for side in order(step - 1):
                z_copy(step - 1, side).wait_send()
                y_copy(step - 1, side).wait_send()
                for q in range(tiles):
                    x_copy(step - 1, side, q).wait_send()
        for side in (LO, HI):
            z_copy(step, side).wait_recv()
            y_copy(step, side).wait_recv()
        interior(step)
        if step == STEPS - 1:
            for cell in range(1, cells - 1):
                finished(cell)
        for side in order(step):
            for q in range(tiles):
                x_copy(step, side, q).wait_recv()
                edge(step, 1 - side, q)
                if step < STEPS - 1:
                    x_copy(step + 1, 1 - side, q).start()
            if step == STEPS - 1:
                finished(0 if side == HI else cells - 1)
        if step < STEPS - 1:
            for side in (LO, HI):
                z_copy(step + 1, side).start()
                y_copy(step + 1, side).start()

    for side in order(STEPS - 1):
        z_copy(STEPS - 1, side).wait_send()
        y_copy(STEPS - 1, side).wait_send()
        for q in range(tiles):
            x_copy(STEPS - 1, side, q).wait_send()

    count = float(planes * rows)
    for cell in range(cells):
        for copy in line_copies(cell):
            copy.wait()
        total, square = line[0, cell, 0], line[0, cell, 1]
        for r in range(1, rows):
            total, square = total + line[r, cell, 0], square + line[r, cell, 1]
        shift = total / count
        stat[0, cell] = GUESS + shift
        stat[1, cell] = lax.rsqrt(square / count - shift * shift + EPS)
    stat_copy = pltpu.make_async_copy(stat, stat_hbm, own.at[0])
    stat_copy.start()
    for cell in range(cells):
        out_copy(cell).wait()
    stat_copy.wait()


def rescale(p_ref, stat_ref, scaled_ref, end_ref):
    mean, scale = stat_ref[0], stat_ref[1]

    def plane(j, carry):
        value = p_ref[j]
        end_ref[j] = value
        scaled_ref[j] = (value - mean) * scale
        return carry

    lax.fori_loop(0, p_ref.shape[0], plane, 0)


def shards(sizes, pressure, earlier, speed_square):
    rows = sizes[0]
    planes, cells, depth, members = pressure.shape
    tiles = depth // TILE
    any_space = pl.BlockSpec(memory_space=pl.ANY)
    dma = pltpu.SemaphoreType.DMA
    end, stat = pl.pallas_call(
        functools.partial(leapfrog, sizes),
        out_shape=(
            jax.ShapeDtypeStruct(pressure.shape, jnp.float32),
            jax.ShapeDtypeStruct((2, cells, depth, members), jnp.float32),
        ),
        in_specs=[any_space] * 3,
        out_specs=(any_space, any_space),
        scratch_shapes=[
            pltpu.VMEM((planes + 2, cells, depth, members), jnp.float32),
            pltpu.VMEM((planes + 2, cells, depth, members), jnp.float32),
            pltpu.VMEM((planes, cells, depth, members), jnp.float32),
            pltpu.VMEM((STEPS, 2, planes, depth, members), jnp.float32),
            pltpu.VMEM((STEPS, 2, planes, cells, TILE, members), jnp.float32),
            pltpu.VMEM((rows, cells, 2, depth, members), jnp.float32),
            pltpu.VMEM((2, cells, depth, members), jnp.float32),
            dma((STEPS, 2, tiles)), dma((STEPS, 2, tiles)),
            dma((STEPS, 2)), dma((STEPS, 2)),
            dma((STEPS, 2)), dma((STEPS, 2)),
            dma((cells, rows - 1)), dma((cells, rows - 1)),
            dma((3,)), dma((cells,)),
        ],
        compiler_params=pltpu.CompilerParams(
            collective_id=0, has_side_effects=True, vmem_limit_bytes=60 * 1024 * 1024
        ),
    )(pressure, earlier, speed_square)

    block = (TILE, cells, depth, members)
    spec = pl.BlockSpec(block, lambda j: (j, 0, 0, 0))
    return pl.pallas_call(
        rescale,
        grid=(planes // TILE,),
        out_shape=(jax.ShapeDtypeStruct(pressure.shape, jnp.float32),) * 2,
        in_specs=[spec, pl.BlockSpec((2, cells, depth, members), lambda j: (0, 0, 0, 0))],
        out_specs=(spec, spec),
    )(end, stat)


def solution(mesh):
    spec = P("rows", "cols", "slabs", None)
    sizes = tuple(mesh.shape[name] for name in ("rows", "cols", "slabs"))
    return jax.shard_map(functools.partial(shards, sizes), mesh=mesh,
                         in_specs=(spec,) * 3, out_specs=(spec,) * 2, check_vma=False)
```

time: 518 us -> 298 us (0.58)
  waiting for transfers between devices: 347 us -> 0 us
  Pallas kernels: 0 us -> 297 us
  other arithmetic: 124 us -> 0 us
  starting transfers between devices: 21.9 us -> 0 us
  between operations: 14.2 us -> 0.64 us
  local copies, waits for them, and re-layouts: 10.6 us -> 0 us
    ppermute x18 -> x0, waiting for transfers between devices: 312 us -> none  [the longest x9 156 us: padded_2(): before = lax.ppermute(last, axis, up)]
    pallas_call x0 -> x2, Pallas kernels: none -> 297 us  [the longest x1 283 us: shards(): pl.pallas_call(functools.partial(leapfrog, sizes), out_shape=(jax.ShapeDt...]
    add x2 -> x0, other arithmetic: 68.1 us -> none  [one_step(): return 2.0 * middle - before + speed_square * spread]
    reduce_sum x1 -> x0, other arithmetic: 38 us -> none  [shards(): jnp.sum(moved, axis=0, keepdims=True)]
    psum x1 -> x0, waiting for transfers between devices: 34.7 us -> none  [shards(): lax.psum((jnp.sum(moved, axis=0, keepdims=True), jnp.sum(moved * moved, a...]
    ppermute x18 -> x0, starting transfers between devices: 21.9 us -> none  [the longest x9 12 us: padded_2(): after = lax.ppermute(initial, axis, down)]
    mul x1 -> x0, other arithmetic: 8.81 us -> none  [shards(): scaled_field = centred * lax.rsqrt(line_variance + 0.0001)]
    slice x5 -> x0, other arithmetic: 8.18 us -> none  [padded_2(): last = lax.slice_in_dim(shard, length - width, length, axis=dim)]
  transfers between devices with their start and end apart: 19 -> 0, of which waited for: 16 -> 0; matrix products, arithmetic and copies ran while one was open for 1% -> 0% of each run, Pallas kernels for 0% -> 0%
where the time goes in v1:
time: 298 us
  Pallas kernels  297 us (100%)
    pallas_call x1, Pallas kernels, shards(): pl.pallas_call(functools.partial(leapfrog, sizes), out_shape=(jax.ShapeDt...  283 us
    pallas_call x1, Pallas kernels, shards(): pl.pallas_call(rescale, grid=(planes // TILE,), out_shape=(jax.ShapeDtype...  13.6 us

profile of v1, /device:TPU:0, one launch (start us, length us, event | category | flops | bytes accessed | tf_op | source)
XLA Modules:
  0.0 297.7 jit_solution(749012972354682089)
XLA Ops:
  0.6 283.4 %shard_map.50 = (f32[128,4,32,128]{3,2,1,0:T(8,128)}, f32[2,4,32,128]{3,2,1,0:T(8,128)}) custom-call(f32[128,4,32,128]{3,2,1,0:T(8,128)} %p_hbm.1, f32[128,4,32,128]{3,2,1,0:T(8,128)} %e_hbm.1, f32[128,4,32,128]{3,2,1,0:T(8,128)} %s_hbm.1), custom_call_target="tpu_custom_call" | custom-call | tf_op jit(solution)/shard_map/pallas_call | solution.py:225
  284.1 13.6 %shard_map.51 = (f32[128,4,32,128]{3,2,1,0:T(8,128)}, f32[128,4,32,128]{3,2,1,0:T(8,128)}) custom-call(f32[128,4,32,128]{3,2,1,0:T(8,128)} %get-tuple-element.4.p_ref, f32[2,4,32,128]{3,2,1,0:T(8,128)} %get-tuple-element.5.stat_ref), custom_call_target="tpu_custom_call" | custom-call | tf_op jit(solution)/shard_map/pallas_call | solution.py:254

commit v2 on v1

--- a/solution.py
+++ b/solution.py
@@ -15,9 +15,10 @@
 LO, HI = 0, 1
 
 
-def leapfrog(sizes, p_hbm, e_hbm, s_hbm, out_hbm, stat_hbm,
-             even, odd, speed, xh, yh, line, stat,
-             xs, xr, ys, yr, zs, zr, ls, lr, own, out_sem):
+def leapfrog(sizes, p_hbm, e_hbm, s_hbm, end, stat,
+             even, odd, xh, yh, line,
+             xs, xr, ys, yr, zs, zr, ls, lr, own):
+    speed = end
     rows, cols, slabs = sizes
     planes, cells, depth = p_hbm.shape[0], p_hbm.shape[1], p_hbm.shape[2]
     tiles = depth // TILE
@@ -47,6 +48,12 @@
     pl.semaphore_wait(barrier, len(greeted))
 
     fields = (even, odd)
+    count = float(planes * rows)
+
+    def line_copies(cell, q):
+        part = line.at[row, cell, q]
+        return [remote(part, part, ls.at[cell, q, d], lr.at[cell, q, d], device)
+                for d, device in enumerate(peers)]
 
     def remote(src, dst, send, recv, device):
         return pltpu.make_async_remote_copy(
@@ -101,17 +108,20 @@
                       + low(here, padded, part) + high(here, padded, part)
                       + k_low + k_high - 6.0 * mid)
             new = 2.0 * mid - then[padded, cell, part, :] + speed[here, cell, part, :] * spread
-            then[padded, cell, part, :] = new
             if last:
+                end[here, cell, part, :] = new
                 moved = new - GUESS
                 return sums[0] + jnp.sum(moved, axis=0), sums[1] + jnp.sum(moved * moved, axis=0)
+            then[padded, cell, part, :] = new
             return sums
 
         zero = jnp.zeros((TILE, 128), jnp.float32)
         sums = lax.fori_loop(0, planes // TILE, block, (zero, zero) if last else 0)
         if last:
-            line[row, cell, 0, part, :] = sums[0]
-            line[row, cell, 1, part, :] = sums[1]
+            line[row, cell, q, 0] = sums[0]
+            line[row, cell, q, 1] = sums[1]
+            for copy in line_copies(cell, q):
+                copy.start()
 
     def edge(step, side, q):
         now = fields[step % 2]
@@ -133,17 +143,17 @@
 
         lax.fori_loop(1, cells - 1, at, 0)
 
-    def line_copies(cell):
-        return [remote(line.at[row, cell], line.at[row, cell], ls.at[cell, d], lr.at[cell, d], device)
-                for d, device in enumerate(peers)]
-
-    def out_copy(cell):
-        return pltpu.make_async_copy(odd.at[body_planes, cell], out_hbm.at[:, cell], out_sem.at[cell])
-
-    def finished(cell):
-        out_copy(cell).start()
-        for copy in line_copies(cell):
-            copy.start()
+    def settle(cell):
+        for q in range(tiles):
+            for copy in line_copies(cell, q):
+                copy.wait()
+            total, square = line[0, cell, q, 0], line[0, cell, q, 1]
+            for r in range(1, rows):
+                total, square = total + line[r, cell, q, 0], square + line[r, cell, q, 1]
+            shift = total / count
+            part = pl.ds(q * TILE, TILE)
+            stat[0, cell, part, :] = GUESS + shift
+            stat[1, cell, part, :] = lax.rsqrt(square / count - shift * shift + EPS)
 
     for side in order(0):
         for q in range(tiles):
@@ -165,17 +175,15 @@
             z_copy(step, side).wait_recv()
             y_copy(step, side).wait_recv()
         interior(step)
-        if step == STEPS - 1:
-            for cell in range(1, cells - 1):
-                finished(cell)
         for side in order(step):
             for q in range(tiles):
                 x_copy(step, side, q).wait_recv()
                 edge(step, 1 - side, q)
                 if step < STEPS - 1:
                     x_copy(step + 1, 1 - side, q).start()
-            if step == STEPS - 1:
-                finished(0 if side == HI else cells - 1)
+            if step == STEPS - 1 and side == order(step)[0]:
+                for cell in range(1, cells - 1):
+                    settle(cell)
         if step < STEPS - 1:
             for side in (LO, HI):
                 z_copy(step + 1, side).start()
@@ -187,33 +195,31 @@
         for q in range(tiles):
             x_copy(STEPS - 1, side, q).wait_send()
 
-    count = float(planes * rows)
-    for cell in range(cells):
-        for copy in line_copies(cell):
+    for side in order(STEPS - 1):
+        settle(0 if side == HI else cells - 1)
+
+
+def rescale(p_ref, stat_ref, scaled_hbm, end_hbm, scaled, end_sem, scaled_sem):
+    planes, parts = p_ref.shape[0], end_sem.shape[0]
+    each = planes // parts
+    copies = []
+    for c in range(parts):
+        part = pl.ds(c * each, each)
+        copies.append((pltpu.make_async_copy(p_ref.at[part], end_hbm.at[part], end_sem.at[c]),
+                       pltpu.make_async_copy(scaled.at[part], scaled_hbm.at[part], scaled_sem.at[c])))
+
+    for c in range(parts):
+        copies[c][0].start()
+
+        def plane(j, carry):
+            scaled[j] = (p_ref[j] - stat_ref[0]) * stat_ref[1]
+            return carry
+
+        lax.fori_loop(c * each, (c + 1) * each, plane, 0, unroll=2)
+        copies[c][1].start()
+    for pair in copies:
+        for copy in pair:
             copy.wait()
-        total, square = line[0, cell, 0], line[0, cell, 1]
-        for r in range(1, rows):
-            total, square = total + line[r, cell, 0], square + line[r, cell, 1]
-        shift = total / count
-        stat[0, cell] = GUESS + shift
-        stat[1, cell] = lax.rsqrt(square / count - shift * shift + EPS)
-    stat_copy = pltpu.make_async_copy(stat, stat_hbm, own.at[0])
-    stat_copy.start()
-    for cell in range(cells):
-        out_copy(cell).wait()
-    stat_copy.wait()
-
-
-def rescale(p_ref, stat_ref, scaled_ref, end_ref):
-    mean, scale = stat_ref[0], stat_ref[1]
-
-    def plane(j, carry):
-        value = p_ref[j]
-        end_ref[j] = value
-        scaled_ref[j] = (value - mean) * scale
-        return carry
-
-    lax.fori_loop(0, p_ref.shape[0], plane, 0)
 
 
 def shards(sizes, pressure, earlier, speed_square):
@@ -222,41 +228,40 @@
     tiles = depth // TILE
     any_space = pl.BlockSpec(memory_space=pl.ANY)
     dma = pltpu.SemaphoreType.DMA
+    vmem_space = pl.BlockSpec(memory_space=pltpu.VMEM)
     end, stat = pl.pallas_call(
         functools.partial(leapfrog, sizes),
         out_shape=(
-            jax.ShapeDtypeStruct(pressure.shape, jnp.float32),
-            jax.ShapeDtypeStruct((2, cells, depth, members), jnp.float32),
+            pltpu.VMEM(pressure.shape, jnp.float32),
+            pltpu.VMEM((2, cells, depth, members), jnp.float32),
         ),
         in_specs=[any_space] * 3,
-        out_specs=(any_space, any_space),
+        out_specs=(vmem_space, vmem_space),
         scratch_shapes=[
             pltpu.VMEM((planes + 2, cells, depth, members), jnp.float32),
             pltpu.VMEM((planes + 2, cells, depth, members), jnp.float32),
-            pltpu.VMEM((planes, cells, depth, members), jnp.float32),
             pltpu.VMEM((STEPS, 2, planes, depth, members), jnp.float32),
             pltpu.VMEM((STEPS, 2, planes, cells, TILE, members), jnp.float32),
-            pltpu.VMEM((rows, cells, 2, depth, members), jnp.float32),
-            pltpu.VMEM((2, cells, depth, members), jnp.float32),
+            pltpu.VMEM((rows, cells, tiles, 2, TILE, members), jnp.float32),
             dma((STEPS, 2, tiles)), dma((STEPS, 2, tiles)),
             dma((STEPS, 2)), dma((STEPS, 2)),
             dma((STEPS, 2)), dma((STEPS, 2)),
-            dma((cells, rows - 1)), dma((cells, rows - 1)),
-            dma((3,)), dma((cells,)),
+            dma((cells, tiles, rows - 1)), dma((cells, tiles, rows - 1)),
+            dma((3,)),
         ],
         compiler_params=pltpu.CompilerParams(
-            collective_id=0, has_side_effects=True, vmem_limit_bytes=60 * 1024 * 1024
+            collective_id=0, has_side_effects=True, vmem_limit_bytes=46 * 1024 * 1024
         ),
     )(pressure, earlier, speed_square)
 
-    block = (TILE, cells, depth, members)
-    spec = pl.BlockSpec(block, lambda j: (j, 0, 0, 0))
+    parts = 8
     return pl.pallas_call(
         rescale,
-        grid=(planes // TILE,),
         out_shape=(jax.ShapeDtypeStruct(pressure.shape, jnp.float32),) * 2,
-        in_specs=[spec, pl.BlockSpec((2, cells, depth, members), lambda j: (0, 0, 0, 0))],
-        out_specs=(spec, spec),
+        in_specs=[vmem_space, vmem_space],
+        out_specs=(any_space, any_space),
+        scratch_shapes=[pltpu.VMEM(pressure.shape, jnp.float32), dma((parts,)), dma((parts,))],
+        compiler_params=pltpu.CompilerParams(vmem_limit_bytes=24 * 1024 * 1024),
     )(end, stat)
 
 

time: 298 us -> 289 us (0.970)
  Pallas kernels: 297 us -> 289 us
    pallas_call x2, Pallas kernels: 297 us -> 289 us  [the longest x1 283 us: shards(): pl.pallas_call(functools.partial(leapfrog, sizes), out_shape=(pltpu.VMEM(...]
where the time goes in v2:
time: 289 us
  Pallas kernels  289 us (100%)
    pallas_call x1, Pallas kernels, shards(): pl.pallas_call(functools.partial(leapfrog, sizes), out_shape=(pltpu.VMEM(...  283 us
    pallas_call x1, Pallas kernels, shards(): pl.pallas_call(rescale, out_shape=(jax.ShapeDtypeStruct(pressure.shape, j...  5.96 us

profile of v2, /device:TPU:0, one launch (start us, length us, event | category | flops | bytes accessed | tf_op | source)
XLA Modules:
  0.0 289.3 jit_solution(17567628987237482989)
XLA Ops:
  0.6 282.7 %shard_map.50 = (f32[128,4,32,128]{3,2,1,0:T(8,128)S(1)}, f32[2,4,32,128]{3,2,1,0:T(8,128)S(1)}) custom-call(f32[128,4,32,128]{3,2,1,0:T(8,128)} %p_hbm.1, f32[128,4,32,128]{3,2,1,0:T(8,128)} %e_hbm.1, f32[128,4,32,128]{3,2,1,0:T(8,128)} %s_hbm.1), custom_call_target="tpu_custom_call" | custom-call | tf_op jit(solution)/shard_map/pallas_call | solution.py:232
  283.3 6.0 %shard_map.51 = (f32[128,4,32,128]{3,2,1,0:T(8,128)}, f32[128,4,32,128]{3,2,1,0:T(8,128)}) custom-call(f32[128,4,32,128]{3,2,1,0:T(8,128)S(1)} %get-tuple-element.4.p_ref, f32[2,4,32,128]{3,2,1,0:T(8,128)S(1)} %get-tuple-element.5.stat_ref), custom_call_target="tpu_custom_call" | custom-call | tf_op jit(solution)/shard_map/pallas_call | solution.py:258
